TPU v7x, 256 devices: a whole 4x4x8 slice. The times are simulated.
256 devices in a mesh: front: 16 (over z, core), row: 4 (over y), col: 4 (over x).
Axes of the slice: x: 4, y: 4, z: 8, core: 2. Of those that a mesh axis runs over, the one named last changes fastest.
Arguments:
- child_blocks: bfloat16 [131072, 8192], P(('front', 'row'), 'col'), may hold values from -0.0625 to 0.0625
- sketch: bfloat16 [8192, 512], P('col'), may hold values from -6 to 6
- block_map: int32 [16, 64], P('front'), may hold values from 0 to 95, as said below
Outputs:
- parent_basis: float32 [512, 49152], P('col', ('front', 'row'))
Inputs may be any that keep to these rules, and one draw needn't show every extreme that they name: `block_map`: each row lists 8192 / 128 different parent blocks in increasing order.
All inputs are finite; a program needn't handle non-finite values.
Results may differ from a plain program's by a relative error of at most 0.0003.
Values sent between devices are 32-bit elements; how exact they have to be, the bound alone decides.
A program may use at most 128 MiB of HBM per device.

v0:
```python
import jax
import jax.numpy as jnp
from jax import lax
from jax.sharding import PartitionSpec as P

P_SIZE = 12288
BLK = 128


def from_partner(array, axis, stride):
    return lax.ppermute(array, axis, [(i, i ^ 1 << stride) for i in range(lax.axis_size(axis))])


def from_everyone(array, axis):
    count = lax.axis_size(axis)
    return lax.all_to_all(
        jnp.broadcast_to(array[None], (count, *array.shape)), axis, 0, 0, tiled=True
    )


def in_order(pieces, dim):
    pieces = jnp.moveaxis(pieces, 0, dim)
    dims = pieces.shape
    return pieces.reshape(*dims[:dim], dims[dim] * dims[dim + 1], *dims[dim + 2 :])


def gathered_copies(array, axis, dim):
    pieces = from_everyone(array, axis)
    return in_order(pieces, dim)


def of_everyone(array, axis):
    everything = from_everyone(array, axis)
    return jnp.sum(everything, axis=0)


def shards(child_blocks, sketch, block_map):
    siblings = min(4, lax.axis_size("front"))
    levels = siblings.bit_length() - 1
    front_here = lax.axis_index("front")
    row_here = lax.axis_index("row")
    row_count = lax.axis_size("row")
    sketch_part = lax.psum_scatter(
        lax.dot_general(
            sketch, child_blocks, (((0,), (1,)), ((), ())), preferred_element_type=jnp.float32
        ),
        "col",
        scatter_dimension=0,
        tiled=True,
    )
    width_here = sketch_part.shape[0]
    parent_blocks = P_SIZE // BLK
    share_blocks = parent_blocks // (siblings * row_count)
    rows_all = lax.all_gather(sketch_part, "row", axis=1, tiled=True)
    maps_all = block_map[0]
    block_count = maps_all.shape[0]
    capacity = min(share_blocks, block_count)
    blocks_all = rows_all.reshape(width_here, block_count, BLK)
    dest_share = maps_all // share_blocks
    dest_sibling = dest_share // row_count
    dest_row = dest_share % row_count
    place_plus = (maps_all % share_blocks + 1).astype(jnp.float32)
    sibling_here = front_here % siblings
    slot_ids = jnp.arange(capacity, dtype=jnp.int32)
    place_ids = jnp.arange(share_blocks, dtype=jnp.int32).astype(jnp.float32)
    share = jnp.zeros((width_here, share_blocks, BLK), jnp.float32)
    for offset_bits in range(siblings):
        target_sibling = jnp.bitwise_xor(sibling_here, offset_bits)
        wanted = (dest_sibling == target_sibling) & (dest_row == row_here)
        slot = jnp.cumsum(wanted.astype(jnp.int32)) - 1
        select = (wanted[:, None] & (slot[:, None] == slot_ids[None, :])).astype(jnp.float32)
        packed = jnp.einsum("cbk,bj->cjk", blocks_all, select, precision=lax.Precision.HIGHEST)
        places = jnp.dot(place_plus, select, precision=lax.Precision.HIGHEST) - 1.0
        for bit_level in range(levels):
            if offset_bits >> bit_level & 1:
                packed, places = from_partner((packed, places), "front", bit_level)
        landing = (places[:, None] == place_ids[None, :]).astype(jnp.float32)
        share = share + jnp.einsum("cjk,jm->cmk", packed, landing, precision=lax.Precision.HIGHEST)
    share = share.reshape(width_here, share_blocks * BLK)
    columns_all = gathered_copies(share, "col", 0)
    gram = lax.dot_general(
        columns_all, columns_all, (((1,), (1,)), ((), ())), precision=lax.Precision.HIGHEST
    )
    gram = of_everyone(gram, "row")
    for bit_level in range(levels):
        gram = gram + from_partner(gram, "front", bit_level)
    lower = jnp.linalg.cholesky(gram)
    basis = jax.scipy.linalg.solve_triangular(lower, columns_all, lower=True)
    return lax.dynamic_slice_in_dim(basis, lax.axis_index("col") * width_here, width_here, 0)


def solution(mesh):
    placed = (P(("front", "row"), "col"), P("col", None), P("front", None))
    return jax.shard_map(
        shards, mesh=mesh, in_specs=placed, out_specs=P("col", ("front", "row")), check_vma=False
    )
```

profile of v0, /device:TPU:1, one launch (start us, length us, event | category | flops | bytes accessed | tf_op | source)
XLA Modules:
  0.0 437.4 jit_solution(11003192860249560850)
XLA Ops:
  6.5 1.6 copy-done
  8.1 9.6 %fusion.101 = f32[512,2048]{1,0:T(8,128)} fusion(bf16[2048,512]{1,0:T(8,128)(2,1)S(1)} %copy-done, bf16[2048,2048]{1,0:T(8,128)(2,1)} %param.3), kind=kOutput, calls=%fused_computation.178 | convolution fusion | flops 4294967296 | bytes 14680064 | tf_op jit(solution)/shard_map/dot_general | solution.py:44
  17.8 53.2 %reduce-scatter.2.cloned.1.call-done = f32[128,2048]{1,0:T(8,128)} async-done(((f32[512,2048]{1,0:T(8,128)}), f32[128,2048]{1,0:T(8,128)}) %reduce-scatter.2.cloned.1.call-update) | async-done | bytes 1048592 | tf_op jit(solution)/shard_map/reduce_scatter | solution.py:43
  71.8 0.7 collective-permute-start
  72.8 1.3 collective-permute-start.2
  74.8 48.5 %all-gather.2.cloned.1.call-done = f32[128,8192]{1,0:T(8,128)} async-done(((f32[128,2048]{1,0:T(8,128)}), f32[128,8192]{1,0:T(8,128)}) %all-gather.2.cloned.1.call-update) | async-done | bytes 4194320 | tf_op jit(solution)/shard_map/all_gather | solution.py:54
  123.3 2.9 copy.22
  126.2 1.5 convolution_bitcast_fusion.2
  127.7 1.5 convolution_bitcast_fusion.3
  129.1 1.5 convolution_bitcast_fusion
  130.6 0.9 collective-permute-start.1
  131.5 0.6 collective-permute-start.6
  132.1 1.5 convolution_bitcast_fusion.1
  133.6 1.4 collective-permute-start.3
  135.4 0.8 collective-permute-start.4
  136.1 0.8 collective-permute-done.4
  137.1 1.3 collective-permute-start.7
  138.9 7.9 %collective-permute-done.3 = f32[128,6,128]{2,1,0:T(8,128)S(1)} collective-permute-done((f32[128,6,128]{2,1,0:T(8,128)S(1)}, f32[128,6,128]{2,1,0:T(8,128)S(1)}, u32[]{:S(2)}, u32[]{:S(2)}) %collective-permute-start.3) | collective-permute-done | bytes 393248 | tf_op jit(solution)/shard_map/ppermute | solution.py:11
  147.2 10.8 %collective-permute-done.7 = f32[128,6,128]{2,1,0:T(8,128)S(1)} collective-permute-done((f32[128,6,128]{2,1,0:T(8,128)S(1)}, f32[128,6,128]{2,1,0:T(8,128)S(1)}, u32[]{:S(2)}, u32[]{:S(2)}) %collective-permute-start.7) | collective-permute-done | bytes 393248 | tf_op jit(solution)/shard_map/ppermute | solution.py:11
  158.9 22.8 %all_to_all.10 = f32[4,128,768]{2,1,0:T(8,128)S(1)} all-to-all(f32[4,128,768]{2,1,0:T(8,128)S(1)} %broadcast_in_dim.8), channel_id=1, replica_groups=mesh['front'=16,'row'=4,'col'=4] {'col'}, dimensions={0} | all-to-all | bytes 3145728 | tf_op jit(solution)/shard_map/all_to_all | solution.py:16
  181.7 1.2 copy-done.1
  182.9 2.7 fusion.102
  186.2 49.7 %all_to_all.11 = f32[4,512,512]{2,1,0:T(8,128)} all-to-all(f32[4,512,512]{2,1,0:T(8,128)S(1)} %broadcast_in_dim.9), channel_id=1, replica_groups=mesh['front'=16,'row'=4,'col'=4] {'row'}, dimensions={0} | all-to-all | bytes 8388608 | tf_op jit(solution)/shard_map/all_to_all | solution.py:16
  235.9 3.8 reduce_sum.9
  239.6 1.6 copy.20
  241.2 3.6 collective-permute-start.8
  244.8 2.3 collective-permute-done.8
  247.1 1.4 add.217
  248.5 1.5 collective-permute-start.9
  250.0 23.2 %collective-permute-done.9 = f32[512,512]{0,1:T(8,128)} collective-permute-done((f32[512,512]{0,1:T(8,128)S(1)}, f32[512,512]{0,1:T(8,128)}, u32[]{:S(2)}, u32[]{:S(2)}) %collective-permute-start.9) | collective-permute-done | bytes 1048608 | tf_op jit(solution)/shard_map/ppermute | solution.py:11
  273.2 1.7 add.218
  275.0 1.3 copy.21
  276.3 1.4 fusion.10
  277.8 1.0 copy-done.5
  278.7 11.7 %cholesky.104 = f32[128,128]{1,0:T(8,128)S(1)} custom-call(f32[128,128]{1,0:T(8,128)S(1)} %cholesky.266), custom_call_target="Cholesky" | custom-call | tf_op jit(solution)/shard_map/jit(cholesky)/cholesky | solution.py:87
  290.6 9.8 %custom-call.31 = f32[1,128,128]{1,2,0:T(8,128)S(1)} custom-call(f32[1,128,128]{2,1,0:T(8,128)S(1)} %get-tuple-element.39), custom_call_target="InvertDiagBlocksLowerTriangular" | custom-call | tf_op jit(solution)/shard_map/jit(cholesky)/cholesky | solution.py:87
  300.4 1.2 constant_dynamic-update-slice_fusion
  301.7 1.3 slice_subtract_fusion
  303.0 11.7 %cholesky.217 = f32[128,128]{1,0:T(8,128)S(1)} custom-call(f32[128,128]{1,0:T(8,128)S(1)} %cholesky.270), custom_call_target="Cholesky" | custom-call | tf_op jit(solution)/shard_map/jit(cholesky)/cholesky | solution.py:87
  314.7 10.0 %custom-call.32 = f32[1,128,128]{1,2,0:T(8,128)S(1)} custom-call(f32[1,128,128]{2,1,0:T(8,128)S(1)} %get-tuple-element.36), custom_call_target="InvertDiagBlocksLowerTriangular" | custom-call | tf_op jit(solution)/shard_map/jit(cholesky)/cholesky | solution.py:87
  325.0 1.3 slice_subtract_fusion.1
  326.3 11.7 %cholesky.238 = f32[128,128]{1,0:T(8,128)S(1)} custom-call(f32[128,128]{1,0:T(8,128)S(1)} %cholesky.275), custom_call_target="Cholesky" | custom-call | tf_op jit(solution)/shard_map/jit(cholesky)/cholesky | solution.py:87
  338.0 0.7 compare_reduce_fusion.1
  338.8 9.8 %custom-call.33 = f32[1,128,128]{1,2,0:T(8,128)S(1)} custom-call(f32[1,128,128]{2,1,0:T(8,128)S(1)} %get-tuple-element.33), custom_call_target="InvertDiagBlocksLowerTriangular" | custom-call | tf_op jit(solution)/shard_map/jit(cholesky)/cholesky | solution.py:87
  348.8 1.2 slice_subtract_fusion.2
  350.0 11.7 %cholesky.255 = f32[128,128]{1,0:T(8,128)S(1)} custom-call(f32[128,128]{1,0:T(8,128)S(1)} %slice_subtract_fusion.2), custom_call_target="Cholesky" | custom-call | tf_op jit(solution)/shard_map/jit(cholesky)/cholesky | solution.py:87
  362.0 0.6 compare_reduce_fusion
  362.6 0.7 compare_reduce_fusion.2
  365.8 1.1 select_select_fusion
  366.9 14.1 %while.1 = (s32[]{:T(128)}, f32[512,512]{1,0:T(8,128)}, s32[4,2]{0,1:T(2,128)S(1)}, f32[4,128,128]{2,1,0:T(8,128)}, s32[]{:T(128)}) while((s32[]{:T(128)}, f32[512,512]{1,0:T(8,128)}, s32[4,2]{0,1:T(2,128)S(1)}, f32[4,128,128]{2,1,0:T(8,128)}, s32[]{:T(128)}) %tuple.36), condition=%wide.while_cond, body=%wide.while_body.sunk | while | flops 2 | bytes 132705 | solution.py:88
  367.0 0.6 fusion.125
  367.6 2.9 bitcast_dynamic-update-slice_fusion.2
  370.5 0.6 fusion.125
  371.1 2.9 bitcast_dynamic-update-slice_fusion.2
  374.1 0.6 fusion.125
  374.7 2.9 bitcast_dynamic-update-slice_fusion.2
  377.6 0.6 fusion.125
  378.2 2.8 bitcast_dynamic-update-slice_fusion.2
  381.0 40.1 %custom-call.34 = f32[4,128,128]{1,2,0:T(8,128)S(1)} custom-call(f32[4,128,128]{2,1,0:T(8,128)} %get-tuple-element.12), custom_call_target="InvertDiagBlocksLowerTriangular" | custom-call | tf_op jit(solution)/shard_map/jit(_solve_triangular)/triangular_solve | solution.py:88
  421.2 1.6 fusion.17
  422.8 1.5 convolution_subtract_fusion.1
  424.9 1.5 convolution_subtract_fusion.2
  426.9 1.8 convolution_subtract_fusion
  429.2 0.9 fusion.16
  (70 shorter events, 7.3 us)
Async XLA Ops:
  6.5 1.6 copy-start
  6.5 64.4 %reduce-scatter.2.cloned.1.call-start = ((), (), s32[]{:S(2)}) async-start(), calls=%async_computation.3 | async-start | bytes 5242880 | tf_op jit(solution)/shard_map/reduce_scatter | solution.py:43
  17.7 53.3 %copy-start.6 = (s32[1,64]{1,0:T(1,128)S(1)}, s32[1,64]{1,0:T(1,128)}, u32[]{:S(2)}) copy-start(s32[1,64]{1,0:T(1,128)} %param.5) | copy-start | bytes 772
  17.7 105.5 %all-gather.2.cloned.1.call-start = ((), (), s32[]{:S(2)}) async-start(), calls=%async_computation.4 | async-start | bytes 5242880 | tf_op jit(solution)/shard_map/all_gather | solution.py:54
  71.8 63.6 %collective-permute-start = (f32[6]{0:T(128)S(1)}, f32[6]{0:T(128)S(1)}, u32[]{:S(2)}, u32[]{:S(2)}) collective-permute-start(f32[6]{0:T(128)S(1)} %fusion.7), channel_id=1, source_target_pairs={{0,16},{16,0},{32,48},{48,32},{64,80},{80,64},{96,112},{112,96},{1... | collective-permute-start | bytes 80 | tf_op jit(solution)/shard_map/ppermute | solution.py:11
  72.8 66.0 %collective-permute-start.2 = (f32[6]{0:T(128)S(1)}, f32[6]{0:T(128)S(1)}, u32[]{:S(2)}, u32[]{:S(2)}) collective-permute-start(f32[6]{0:T(128)S(1)} %fusion.8), channel_id=1, source_target_pairs={{0,32},{16,48},{32,0},{48,16},{64,96},{80,112},{96,64},{112,80},{1... | collective-permute-start | bytes 80 | tf_op jit(solution)/shard_map/ppermute | solution.py:11
  130.6 7.8 %collective-permute-start.1 = (f32[128,6,128]{2,1,0:T(8,128)S(1)}, f32[128,6,128]{2,1,0:T(8,128)S(1)}, u32[]{:S(2)}, u32[]{:S(2)}) collective-permute-start(f32[128,6,128]{2,1,0:T(8,128)S(1)} %convolution_bitcast_fusion.2), channel_id=1, source_target_pairs={{0,16},{16,0},{32,48},{48,32},{64,80},{80,64},{96,112},{112,96},{1... | collective-permute-start | bytes 1179656 | tf_op jit(solution)/shard_map/ppermute | solution.py:11
  131.5 5.6 %collective-permute-start.6 = (f32[128,6,128]{2,1,0:T(8,128)S(1)}, f32[128,6,128]{2,1,0:T(8,128)S(1)}, u32[]{:S(2)}, u32[]{:S(2)}) collective-permute-start(f32[128,6,128]{2,1,0:T(8,128)S(1)} %convolution_bitcast_fusion), channel_id=1, source_target_pairs={{0,16},{16,0},{32,48},{48,32},{64,80},{80,64},{96,112},{112,96},{1... | collective-permute-start | bytes 1179656 | tf_op jit(solution)/shard_map/ppermute | solution.py:11
  133.6 13.2 %collective-permute-start.3 = (f32[128,6,128]{2,1,0:T(8,128)S(1)}, f32[128,6,128]{2,1,0:T(8,128)S(1)}, u32[]{:S(2)}, u32[]{:S(2)}) collective-permute-start(f32[128,6,128]{2,1,0:T(8,128)S(1)} %convolution_bitcast_fusion.1), channel_id=1, source_target_pairs={{0,32},{16,48},{32,0},{48,16},{64,96},{80,112},{96,64},{112,80},{1... | collective-permute-start | bytes 1179656 | tf_op jit(solution)/shard_map/ppermute | solution.py:11
  135.4 1.6 collective-permute-start.4
  136.9 10.2 %collective-permute-start.5 = (f32[6]{0:T(128)S(1)}, f32[6]{0:T(128)S(1)}, u32[]{:S(2)}, u32[]{:S(2)}) collective-permute-start(f32[6]{0:T(128)S(1)} %collective-permute-done.4), channel_id=1, source_target_pairs={{0,32},{16,48},{32,0},{48,16},{64,96},{80,112},{96,64},{112,80},{1... | collective-permute-start | bytes 80 | tf_op jit(solution)/shard_map/ppermute | solution.py:11
  137.1 20.9 %collective-permute-start.7 = (f32[128,6,128]{2,1,0:T(8,128)S(1)}, f32[128,6,128]{2,1,0:T(8,128)S(1)}, u32[]{:S(2)}, u32[]{:S(2)}) collective-permute-start(f32[128,6,128]{2,1,0:T(8,128)S(1)} %collective-permute-done.6), channel_id=1, source_target_pairs={{0,32},{16,48},{32,0},{48,16},{64,96},{80,112},{96,64},{112,80},{1... | collective-permute-start | bytes 1179656 | tf_op jit(solution)/shard_map/ppermute | solution.py:11
  181.7 1.2 copy-start.1
  241.2 3.6 copy-start.4
  241.2 5.9 %collective-permute-start.8 = (f32[512,512]{0,1:T(8,128)S(1)}, f32[512,512]{0,1:T(8,128)S(1)}, u32[]{:S(2)}, u32[]{:S(2)}) collective-permute-start(f32[512,512]{0,1:T(8,128)S(1)} %copy.20), channel_id=1, source_target_pairs={{0,16},{16,0},{32,48},{48,32},{64,80},{80,64},{96,112},{112,96},{1... | collective-permute-start | bytes 3145736 | tf_op jit(solution)/shard_map/ppermute | solution.py:11
  248.5 1.6 copy-start.3
  248.5 24.7 %collective-permute-start.9 = (f32[512,512]{0,1:T(8,128)S(1)}, f32[512,512]{0,1:T(8,128)}, u32[]{:S(2)}, u32[]{:S(2)}) collective-permute-start(f32[512,512]{0,1:T(8,128)S(1)} %add.217), channel_id=1, source_target_pairs={{0,32},{16,48},{32,0},{48,16},{64,96},{80,112},{96,64},{112,80},{1... | collective-permute-start | bytes 3145736 | tf_op jit(solution)/shard_map/ppermute | solution.py:11
  277.7 1.0 copy-start.5
  421.2 3.7 copy-start.2
Sparse Core Ops, SparseCore 0:
  17.9 53.0 reduce-scatter.1
  72.8 50.4 all-gather.1
where the time goes:
time: 446 us; the launch traced here: 437 us
  waiting for transfers between devices  147 us (33%)
  other arithmetic  130 us (29%)
  blocking collectives  72.5 us (16%)
  matrix products  33.8 us (8%)
  local copies, waits for them, and re-layouts  25.1 us (6%)
  between operations  16.9 us (4%)
  starting transfers between devices  12.2 us (3%)
    another operation x14, other arithmetic, shards(): lower = jnp.linalg.cholesky(gram)  78.7 us
    all_to_all x2, blocking collectives, from_everyone(): lax.all_to_all(jnp.broadcast_to(array[None], (count, *array.shape)), axis...  72.5 us
    reduce_scatter x1, waiting for transfers between devices, shards(): lax.psum_scatter(lax.dot_general(sketch, child_blocks, (((0,), (1,)), (()...  53.2 us
    all_gather x1, waiting for transfers between devices, shards(): rows_all = lax.all_gather(sketch_part, 'row', axis=1, tiled=True)  48.5 us
    ppermute x10, waiting for transfers between devices, from_partner(): lax.ppermute(array, axis, [(i, i ^ 1 << stride) for i in range(lax.axis_s...  45 us
    another operation x4, other arithmetic, shards(): basis = jax.scipy.linalg.solve_triangular(lower, columns_all, lower=True)  42.2 us
    another operation x12, local copies, waits for them, and re-layouts  14.1 us
    ppermute x10, starting transfers between devices, from_partner(): lax.ppermute(array, axis, [(i, i ^ 1 << stride) for i in range(lax.axis_s...  12.2 us
  transfers between devices with their start and end apart: 12, of which 7 were waited for; matrix products, arithmetic and copies ran while one was open for 3% of the time, Pallas kernels for 0%

commit v1 on v0

v1 whole, which is shorter than its diff:
```python
import jax
import jax.numpy as jnp
from jax import lax
from jax.experimental import pallas as pl
from jax.experimental.pallas import tpu as pltpu
from jax.sharding import PartitionSpec as P

MESH = pl.DeviceIdType.MESH
HIGHEST = lax.Precision.HIGHEST
VMEM = pl.BlockSpec(memory_space=pltpu.VMEM)
BLK = 128
PARENT_BLOCKS = 96
SUB = 32
SRC = 16
OWN = 6
STAGES = [(q, g) for q in range(4) for g in range(2)]
SLICE_OF_STEP = ((0, 2, 1), (1, 2, 0))


def remote(src, dst, send, recv, **where):
    return pltpu.make_async_remote_copy(
        src_ref=src, dst_ref=dst, send_sem=send, recv_sem=recv, device_id=where, device_id_type=MESH
    )


def meet(peers):
    barrier = pltpu.get_barrier_semaphore()
    for where in peers:
        pl.semaphore_signal(barrier, inc=1, device_id=where, device_id_type=MESH)
    pl.semaphore_wait(barrier, len(peers))


def around(axis):
    here = lax.axis_index(axis)
    return here, [lax.rem(here + step, 4) for step in range(4)]


def flip(front, bits):
    low = lax.rem(front, 4)
    core, half = lax.rem(low, 2), low // 2
    if bits & 1:
        core = 1 - core
    if bits & 2:
        half = 1 - half
    return front - low + 2 * half + core


def share_kernel(
    a_hbm, om_hbm, map_ref, s_ref,
    a_v, om_v, part, xr, ys, yr, tab_v, tab_s,
    a_sem, om_sem, tab_sem, tab_ss, tab_rs, x_ss, x_rs, c_ss, c_rs, z_ss, z_rs, f_ss, f_rs, y_ss, y_rs,
    *gats,
):
    front = lax.axis_index("front")
    sibling = lax.rem(front, 4)
    row, rows = around("row")
    col, cols = around("col")
    near = [flip(front, bits) for bits in range(4)]
    pending = []

    om_copy = pltpu.make_async_copy(om_hbm, om_v, om_sem)
    om_copy.start()
    a_copies = []
    for i, s in enumerate((cols[3], cols[1], cols[2], col)):
        copy = pltpu.make_async_copy(
            a_hbm.at[:, pl.ds(pl.multiple_of(s * SUB, SUB), SUB), :], a_v.at[i], a_sem.at[i]
        )
        copy.start()
        a_copies.append(copy)

    meet(
        [{"col": cols[1]}, {"col": cols[3]}]
        + [{"row": rows[k]} for k in (1, 2, 3)]
        + [{"front": near[k]} for k in (1, 2, 3)]
    )

    lane = lax.broadcasted_iota(jnp.int32, (8, BLK), 1)
    table = jnp.full((8, BLK), SRC, jnp.int32)
    for b in range(SRC):
        table = jnp.where(lane == map_ref[0, row * SRC + b], b, table)
    tab_v[0] = table
    tab_copies = []
    for k in (1, 2, 3):
        copy = remote(tab_v.at[0], tab_v.at[k], tab_ss.at[k - 1], tab_rs.at[k - 1], front=near[k])
        copy.start()
        tab_copies.append(copy)
    for gat in gats:
        for k in range(4):
            gat[k, SRC] = jnp.zeros((8, BLK), jnp.float32)

    def multiply(i, h):
        part[i, :, :, 256 * h : 256 * h + 256] = jnp.dot(
            a_v[i].reshape(SRC * SUB, a_v.shape[-1]),
            om_v[:, 256 * h : 256 * h + 256],
            preferred_element_type=jnp.float32,
        ).reshape(SRC, SUB, 256)

    def piece(t, d, i):
        q, g = STAGES[t]
        lo = 256 * d + BLK * g
        return (i, slice(None), slice(8 * q, 8 * q + 8), slice(lo, lo + BLK))

    x_copy, c_copy, z_copy, f_copy, y_copy = {}, {}, {}, {}, {}

    def send_x(t, d, step):
        copy = remote(
            part.at[piece(t, d, SLICE_OF_STEP[d][step])], xr.at[t, d, step],
            x_ss.at[t, d, step], x_rs.at[t, d, step], col=cols[1] if d == 0 else cols[3],
        )
        copy.start()
        x_copy[t, d, step] = copy
        pending.append(copy)

    def pass_x(t, d, step):
        x_copy[t, d, step - 1].wait_recv()
        at = piece(t, d, SLICE_OF_STEP[d][step])
        part[at] = part[at] + xr[t, d, step - 1]
        send_x(t, d, step)

    def finish_x(t, d):
        x_copy[t, d, 2].wait_recv()
        gat = gats[2 * t + d]
        gat[0, :SRC] = part[piece(t, d, 3)] + xr[t, d, 2]
        z = remote(gat.at[0, :SRC], gat.at[2, :SRC], z_ss.at[t, d], z_rs.at[t, d], front=near[2])
        z.start()
        c = remote(gat.at[0, :SRC], gat.at[1, :SRC], c_ss.at[t, d], c_rs.at[t, d], front=near[1])
        c.start()
        z_copy[t, d], c_copy[t, d] = z, c
        pending.extend((z, c))

    def forward_z(t, d):
        z_copy[t, d].wait_recv()
        gat = gats[2 * t + d]
        copy = remote(gat.at[2, :SRC], gat.at[3, :SRC], f_ss.at[t, d], f_rs.at[t, d], front=near[1])
        copy.start()
        f_copy[t, d] = copy
        pending.append(copy)

    def merge(t, d):
        c_copy[t, d].wait_recv()
        f_copy[t, d].wait_recv()
        gat = gats[2 * t + d]
        for j in range(4 * OWN):
            at = sibling * (4 * OWN) + j
            ys[t, d, j] = (gat[0, tab_s[0, 0, at]] + gat[1, tab_s[1, 0, at]]) + (
                gat[2, tab_s[2, 0, at]] + gat[3, tab_s[3, 0, at]]
            )
        for k in (1, 2, 3):
            copy = remote(
                ys.at[t, d, pl.ds(OWN * rows[k], OWN)], yr.at[t, d, k - 1],
                y_ss.at[t, d, k - 1], y_rs.at[t, d, k - 1], row=rows[k],
            )
            copy.start()
            y_copy[t, d, k] = copy
            pending.append(copy)

    def finish_y(t, d):
        for k in (1, 2, 3):
            y_copy[t, d, k].wait_recv()
        _, _, at_rows, at_cols = piece(t, d, 0)
        s_ref[:, at_rows, at_cols] = (ys[t, d, pl.ds(OWN * row, OWN)] + yr[t, d, 0]) + (
            yr[t, d, 1] + yr[t, d, 2]
        )

    om_copy.wait()
    a_copies[0].wait()
    multiply(0, 0)
    send_x(0, 0, 0)
    send_x(1, 0, 0)
    a_copies[1].wait()
    multiply(1, 1)
    send_x(0, 1, 0)
    send_x(1, 1, 0)
    send_x(2, 0, 0)
    send_x(2, 1, 0)
    a_copies[2].wait()
    a_copies[3].wait()
    for i, h in ((2, 0), (2, 1), (1, 0), (0, 1), (3, 0), (3, 1)):
        multiply(i, h)
    for copy in tab_copies:
        copy.wait()
    tab_copy = pltpu.make_async_copy(tab_v, tab_s, tab_sem)
    tab_copy.start()
    tab_copy.wait()

    count = len(STAGES)
    for tick in range(1, count + 6):
        for action, lag in (
            (lambda t, d: pass_x(t, d, 1), 1),
            (lambda t, d: pass_x(t, d, 2), 2),
            (finish_x, 3),
            (lambda t, d: send_x(t, d, 0), -2),
            (forward_z, 4),
            (merge, 5),
            (finish_y, 6),
        ):
            t = tick - lag
            if t in range(count) and not (lag == -2 and t < 3):
                for d in (0, 1):
                    action(t, d)
    for copy in pending:
        copy.wait_send()


def gram_kernel(
    s_ref, g_ref, all_ref,
    mine, r1, a1, r2, a2, r3, a3, r4,
    c_ss, c_rs, y_ss, y_rs, z_ss, z_rs, x_ss, x_rs, b_ss, b_rs, e_ss, e_rs, s_ss, s_rs, w_ss, w_rs,
):
    front = lax.axis_index("front")
    core = lax.rem(front, 2)
    row, rows = around("row")
    col, cols = around("col")
    near = [flip(front, bits) for bits in range(4)]
    half = 5 * BLK
    fourth = half // 4
    meet(
        [{"col": cols[k]} for k in (1, 2, 3)]
        + [{"row": rows[k]} for k in (1, 2, 3)]
        + [{"front": near[k]} for k in (1, 2)]
    )
    shared = []
    for d in (0, 1):
        copy = remote(s_ref, all_ref.at[:, col], s_ss.at[d], s_rs.at[d], col=cols[1] if d == 0 else cols[3])
        copy.start()
        shared.append(copy)
    all_ref[:, col] = s_ref[...]

    s = s_ref[...].reshape(OWN * SUB, 4 * BLK)
    at = 0
    for i in range(4):
        panel = lax.dot_general(
            s[:, BLK * i : BLK * i + BLK], s[:, BLK * i :], (((0,), (0,)), ((), ())),
            precision=HIGHEST, preferred_element_type=jnp.float32,
        )
        for k in range(4 - i):
            mine[at : at + BLK] = panel[:, BLK * k : BLK * k + BLK]
            at += BLK
    keep = pl.ds(pl.multiple_of(half * core, BLK), half)
    give = pl.ds(pl.multiple_of(half * (1 - core), BLK), half)
    c_copy = remote(mine.at[give], r1, c_ss, c_rs, front=near[1])
    c_copy.start()
    c_copy.wait_recv()
    a1[...] = mine[keep] + r1[...]
    y_copies = []
    for k in (1, 2, 3):
        copy = remote(
            a1.at[pl.ds(pl.multiple_of(fourth * rows[k], 8), fourth)], r2.at[k - 1],
            y_ss.at[k - 1], y_rs.at[k - 1], row=rows[k],
        )
        copy.start()
        y_copies.append(copy)
    for copy in y_copies:
        copy.wait_recv()
    a2[...] = (a1[pl.ds(pl.multiple_of(fourth * row, 8), fourth)] + r2[0]) + (r2[1] + r2[2])
    z_copy = remote(a2, r3, z_ss, z_rs, front=near[2])
    z_copy.start()
    for copy in shared:
        copy.wait_recv()
    passed = []
    for d in (0, 1):
        block = all_ref.at[:, cols[3] if d == 0 else cols[1], 16 * d : 16 * d + 16]
        copy = remote(block, block, w_ss.at[d], w_rs.at[d], col=cols[1] if d == 0 else cols[3])
        copy.start()
        passed.append(copy)
    z_copy.wait_recv()
    a3[...] = a2[...] + r3[...]
    x_copies = []
    for k in (1, 2, 3):
        copy = remote(a3, r4.at[k - 1], x_ss.at[k - 1], x_rs.at[k - 1], col=cols[k])
        copy.start()
        x_copies.append(copy)
    for copy in x_copies:
        copy.wait_recv()
    mid = pl.ds(pl.multiple_of(half * core + fourth * row, 8), fourth)
    g_ref[mid] = (a3[...] + r4[0]) + (r4[1] + r4[2])
    b_copies = []
    for k in (1, 2, 3):
        copy = remote(g_ref.at[mid], g_ref.at[mid], b_ss.at[k - 1], b_rs.at[k - 1], row=rows[k])
        copy.start()
        b_copies.append(copy)
    for copy in b_copies:
        copy.wait_recv()
    e_copy = remote(g_ref.at[keep], g_ref.at[keep], e_ss, e_rs, front=near[1])
    e_copy.start()
    e_copy.wait_recv()
    for copy in passed:
        copy.wait_recv()
    for copy in [c_copy, *y_copies, z_copy, *x_copies, *b_copies, e_copy, *shared, *passed]:
        copy.wait_send()


def factor_inverse(read, write):
    sub = lax.broadcasted_iota(jnp.int32, (8, BLK), 0)
    lane = lax.broadcasted_iota(jnp.int32, (8, BLK), 1)
    count = BLK // 8
    upper = [read(i) for i in range(count)]
    inverse = [jnp.where(lane == sub + 8 * i, 1.0, 0.0).astype(jnp.float32) for i in range(count)]

    def spread(block, k):
        return jnp.broadcast_to(block[k : k + 1, :], (8, BLK))

    for j in range(count):
        below = range(j, count)
        column = {
            i: [jnp.broadcast_to(upper[i][:, 8 * j + k : 8 * j + k + 1], (8, BLK)) for k in range(8)]
            for i in below
        }
        lower = {i: [] for i in below}
        rest, solved = upper[j], inverse[j]
        u_rows, w_rows = [], []
        for k in range(8):
            scale = lax.rsqrt(spread(column[j][k], k))
            for i in below:
                lower[i].append(column[i][k] * scale)
            u_row, w_row = spread(rest, k) * scale, spread(solved, k) * scale
            u_rows.append(u_row)
            w_rows.append(w_row)
            under = jnp.where(sub > k, lower[j][k], 0.0)
            solved = jnp.where(sub == k, w_row, solved - under * w_row)
            rest = rest - under * u_row
            for later in range(k + 1, 8):
                factor = spread(lower[j][k], later)
                for i in below:
                    column[i][later] = column[i][later] - lower[i][k] * factor
        write(j, solved)
        for i in range(j + 1, count):
            for k in range(8):
                upper[i] = upper[i] - lower[i][k] * u_rows[k]
                inverse[i] = inverse[i] - lower[i][k] * w_rows[k]


def basis_kernel(g_ref, all_ref, out_ref, a, v):
    def dot(x, y, dims):
        return lax.dot_general(x, y, (dims, ((), ())), precision=HIGHEST, preferred_element_type=jnp.float32)

    at = 0
    for i in range(4):
        for k in range(i, 4):
            a[i, :, BLK * k : BLK * k + BLK] = g_ref[at : at + BLK]
            at += BLK
    v[...] = jnp.zeros_like(v)
    for j in range(4):
        here = slice(BLK * j, BLK * j + BLK)

        def read(i):
            return a[j, 8 * i : 8 * i + 8, here]

        def write(i, rows):
            v[j, 8 * i : 8 * i + 8, here] = rows

        factor_inverse(read, write)
        w = v[j, :, here]
        if j:
            v[j, :, : BLK * j] = dot(w, v[j, :, : BLK * j], ((1,), (0,)))
        if j < 3:
            u = dot(w, a[j, :, BLK * (j + 1) :], ((1,), (0,)))
            for i in range(j + 1, 4):
                left = u[:, BLK * (i - j - 1) : BLK * (i - j)]
                a[i, :, BLK * i :] = a[i, :, BLK * i :] - dot(left, u[:, BLK * (i - j - 1) :], ((0,), (0,)))
                v[i, :, : BLK * (j + 1)] = v[i, :, : BLK * (j + 1)] - dot(
                    left, v[j, :, : BLK * (j + 1)], ((0,), (0,))
                )
    mine = v[lax.axis_index("col")]
    out_ref[...] = dot(mine, all_ref[...].reshape(OWN * BLK, 4 * BLK), ((1,), (1,)))


def shards(child_blocks, sketch, block_map):
    f32, dma = jnp.float32, pltpu.SemaphoreType.DMA
    stages = len(STAGES)
    depth, width = sketch.shape
    share = pl.pallas_call(
        share_kernel,
        out_shape=jax.ShapeDtypeStruct((OWN, SUB, width), f32),
        in_specs=[
            pl.BlockSpec(memory_space=pl.ANY),
            pl.BlockSpec(memory_space=pl.ANY),
            pl.BlockSpec(memory_space=pltpu.SMEM),
        ],
        out_specs=VMEM,
        scratch_shapes=[
            pltpu.VMEM((4, SRC, SUB, depth), jnp.bfloat16),
            pltpu.VMEM((depth, width), jnp.bfloat16),
            pltpu.VMEM((4, SRC, SUB, width), f32),
            pltpu.VMEM((stages, 2, 3, SRC, 8, BLK), f32),
            pltpu.VMEM((stages, 2, 4 * OWN, 8, BLK), f32),
            pltpu.VMEM((stages, 2, 3, OWN, 8, BLK), f32),
            pltpu.VMEM((4, 8, BLK), jnp.int32),
            pltpu.SMEM((4, 8, BLK), jnp.int32),
            dma((4,)), dma, dma, dma((3,)), dma((3,)),
            dma((stages, 2, 3)), dma((stages, 2, 3)),
            dma((stages, 2)), dma((stages, 2)),
            dma((stages, 2)), dma((stages, 2)),
            dma((stages, 2)), dma((stages, 2)),
            dma((stages, 2, 3)), dma((stages, 2, 3)),
        ]
        + [pltpu.VMEM((4, SRC + 1, 8, BLK), f32)] * (2 * stages),
        compiler_params=pltpu.CompilerParams(collective_id=0, has_side_effects=True, vmem_limit_bytes=48 << 20),
        name="share",
    )(child_blocks.reshape(SRC, BLK, depth), sketch, block_map)
    gram, everyone = pl.pallas_call(
        gram_kernel,
        out_shape=(
            jax.ShapeDtypeStruct((10 * BLK, BLK), f32),
            jax.ShapeDtypeStruct((OWN, 4, SUB, width), f32),
        ),
        in_specs=[VMEM],
        out_specs=(VMEM, VMEM),
        scratch_shapes=[
            pltpu.VMEM((10 * BLK, BLK), f32),
            pltpu.VMEM((5 * BLK, BLK), f32),
            pltpu.VMEM((5 * BLK, BLK), f32),
            pltpu.VMEM((3, 5 * BLK // 4, BLK), f32),
            pltpu.VMEM((5 * BLK // 4, BLK), f32),
            pltpu.VMEM((5 * BLK // 4, BLK), f32),
            pltpu.VMEM((5 * BLK // 4, BLK), f32),
            pltpu.VMEM((3, 5 * BLK // 4, BLK), f32),
            dma, dma, dma((3,)), dma((3,)), dma, dma, dma((3,)), dma((3,)),
            dma((3,)), dma((3,)), dma, dma, dma((2,)), dma((2,)), dma((2,)), dma((2,)),
        ],
        compiler_params=pltpu.CompilerParams(collective_id=1, has_side_effects=True),
        name="gram",
    )(share)
    return pl.pallas_call(
        basis_kernel,
        out_shape=jax.ShapeDtypeStruct((BLK, OWN * BLK), f32),
        in_specs=[VMEM, VMEM],
        out_specs=VMEM,
        scratch_shapes=[pltpu.VMEM((4, BLK, 4 * BLK), f32), pltpu.VMEM((4, BLK, 4 * BLK), f32)],
        name="basis",
    )(gram, everyone)


def solution(mesh):
    placed = (P(("front", "row"), "col"), P("col", None), P("front", None))
    return jax.shard_map(
        shards, mesh=mesh, in_specs=placed, out_specs=P("col", ("front", "row")), check_vma=False
    )
```

time: 446 us -> 118 us (0.26); the launches traced: 437 us -> 118 us
  waiting for transfers between devices: 147 us -> 0 us
  other arithmetic: 130 us -> 0 us
  Pallas kernels: 0 us -> 115 us
  blocking collectives: 72.5 us -> 0 us
  matrix products: 33.8 us -> 0 us
  local copies, waits for them, and re-layouts: 25.1 us -> 2.99 us
  between operations: 16.9 us -> 0.03 us
  starting transfers between devices: 12.2 us -> 0 us
    another operation x22 -> x0, other arithmetic: 121 us -> none  [the longest x14 78.7 us: shards(): lower = jnp.linalg.cholesky(gram)]
    pallas_call x0 -> x3, Pallas kernels: none -> 115 us  [the longest x1 61 us: shards(): pl.pallas_call(share_kernel, out_shape=jax.ShapeDtypeStruct((OWN, SUB, wi...]
    all_to_all x2 -> x0, blocking collectives: 72.5 us -> none  [from_everyone(): lax.all_to_all(jnp.broadcast_to(array[None], (count, *array.shape)), axis...]
    reduce_scatter x1 -> x0, waiting for transfers between devices: 53.2 us -> none  [shards(): lax.psum_scatter(lax.dot_general(sketch, child_blocks, (((0,), (1,)), (()...]
    all_gather x1 -> x0, waiting for transfers between devices: 48.5 us -> none  [shards(): rows_all = lax.all_gather(sketch_part, 'row', axis=1, tiled=True)]
    ppermute x10 -> x0, waiting for transfers between devices: 45 us -> none  [from_partner(): lax.ppermute(array, axis, [(i, i ^ 1 << stride) for i in range(lax.axis_s...]
    dot_general x14 -> x0, matrix products: 20.3 us -> none  [the longest x1 9.59 us: shards(): lax.dot_general(sketch, child_blocks, (((0,), (1,)), ((), ())), preferred...]
    another operation x17 -> x0, local copies, waits for them, and re-layouts: 14.3 us -> none
  transfers between devices with their start and end apart: 12 -> 0, of which waited for: 7 -> 0; matrix products, arithmetic and copies ran while one was open for 3% -> 0% of each run, Pallas kernels for 0% -> 0%
where the time goes in v1:
time: 118 us
  Pallas kernels  115 us (97%)
  local copies, waits for them, and re-layouts  2.99 us (3%)
    pallas_call x1, Pallas kernels, shards(): pl.pallas_call(share_kernel, out_shape=jax.ShapeDtypeStruct((OWN, SUB, wi...  61 us
    pallas_call x1, Pallas kernels, shards(): pl.pallas_call(gram_kernel, out_shape=(jax.ShapeDtypeStruct((10 * BLK, BL...  31.6 us
    pallas_call x1, Pallas kernels, shards(): pl.pallas_call(basis_kernel, out_shape=jax.ShapeDtypeStruct((BLK, OWN * B...  22.3 us
    unnamed x6, local copies, waits for them, and re-layouts  2.99 us

profile of v1, /device:TPU:1, one launch (start us, length us, event | category | flops | bytes accessed | tf_op | source)
XLA Modules:
  0.0 118.0 jit_solution(9284936367091615564)
XLA Ops:
  0.0 0.0 copy-start
  0.0 1.6 %copy-done = bf16[2048,512]{1,0:T(8,128)(2,1)S(1)} copy-done((bf16[2048,512]{1,0:T(8,128)(2,1)S(1)}, bf16[2048,512]{1,0:T(8,128)(2,1)}, u32[]{:S(2)}) %copy-start) | copy-done | bytes 2097176
  1.6 0.0 copy-start.2
  1.6 0.7 copy-done.2
  2.2 61.0 %share.1.s_ref = f32[6,32,512]{2,1,0:T(8,128)S(1)} custom-call(bf16[16,128,2048]{2,1,0:T(8,128)(2,1)} %bitcast.1, bf16[2048,512]{1,0:T(8,128)(2,1)S(1)} %copy-done, s32[1,64]{1,0:T(1,128)S(1)} %copy-done.2), custom_call_target="tpu_custom_call" | custom-call | tf_op jit(solution)/shard_map/share/pallas_call | solution.py:372
  63.2 0.0 copy-start.1
  63.2 0.7 copy-done.1
  64.0 31.6 %gram.1 = (f32[1280,128]{1,0:T(8,128)}, f32[6,4,32,512]{3,2,1,0:T(8,128)}) custom-call(f32[6,32,512]{2,1,0:T(8,128)} %copy-done.1), custom_call_target="tpu_custom_call" | custom-call | tf_op jit(solution)/shard_map/gram/pallas_call | solution.py:401
  95.6 22.3 %basis.1 = f32[128,768]{1,0:T(8,128)} custom-call(f32[1280,128]{1,0:T(8,128)} %get-tuple-element.7.g_ref, f32[6,4,32,512]{3,2,1,0:T(8,128)} %get-tuple-element.8.all_ref), custom_call_target="tpu_custom_call" | custom-call | tf_op jit(solution)/shard_map/basis/pallas_call | solution.py:424
Async XLA Ops:
  0.0 1.6 %copy-start = (bf16[2048,512]{1,0:T(8,128)(2,1)S(1)}, bf16[2048,512]{1,0:T(8,128)(2,1)}, u32[]{:S(2)}) copy-start(bf16[2048,512]{1,0:T(8,128)(2,1)} %om_hbm.1) | copy-start | bytes 6291460
  1.6 0.7 copy-start.2
  63.2 0.7 copy-start.1

commit v2 on v0

v2 whole, which is shorter than its diff:
```python
import jax
import jax.numpy as jnp
from jax import lax
from jax.experimental import pallas as pl
from jax.experimental.pallas import tpu as pltpu
from jax.sharding import PartitionSpec as P

MESH = pl.DeviceIdType.MESH
HIGHEST = lax.Precision.HIGHEST
BLK = 128
SUB = 32
SRC = 16
OWN = 6
HALF = 256
STAGES = [(0, 0, 256), (1, 0, 256), (2, 0, 256), (3, 0, 128), (3, 128, 128)]
PARTS = ((0, 4 * BLK), (4 * BLK, 6 * BLK))


def remote(src, dst, send, recv, **where):
    copy = pltpu.make_async_remote_copy(
        src_ref=src, dst_ref=dst, send_sem=send, recv_sem=recv, device_id=where, device_id_type=MESH
    )
    copy.start()
    return copy


def around(axis):
    here = lax.axis_index(axis)
    return here, [lax.rem(here + step, 4) for step in range(4)]


def flip(front, bits):
    low = lax.rem(front, 4)
    core, half = lax.rem(low, 2), low // 2
    if bits & 1:
        core = 1 - core
    if bits & 2:
        half = 1 - half
    return front - low + 2 * half + core


def dot(x, y, dims):
    return lax.dot_general(x, y, (dims, ((), ())), precision=HIGHEST, preferred_element_type=jnp.float32)


def factor_inverse(read, write):
    sub = lax.broadcasted_iota(jnp.int32, (8, BLK), 0)
    lane = lax.broadcasted_iota(jnp.int32, (8, BLK), 1)
    count = BLK // 8
    upper = [read(i) for i in range(count)]
    inverse = [jnp.where(lane == sub + 8 * i, 1.0, 0.0).astype(jnp.float32) for i in range(count)]

    def spread(block, k):
        return jnp.broadcast_to(block[k : k + 1, :], (8, BLK))

    for j in range(count):
        below = range(j, count)
        column = {
            i: [jnp.broadcast_to(upper[i][:, 8 * j + k : 8 * j + k + 1], (8, BLK)) for k in range(8)]
            for i in below
        }
        lower = {i: [] for i in below}
        rest, solved = upper[j], inverse[j]
        u_rows, w_rows = [], []
        for k in range(8):
            scale = lax.rsqrt(spread(column[j][k], k))
            for i in below:
                lower[i].append(column[i][k] * scale)
            u_row, w_row = spread(rest, k) * scale, spread(solved, k) * scale
            u_rows.append(u_row)
            w_rows.append(w_row)
            under = jnp.where(sub > k, lower[j][k], 0.0)
            solved = jnp.where(sub == k, w_row, solved - under * w_row)
            rest = rest - under * u_row
            for later in range(k + 1, 8):
                factor = spread(lower[j][k], later)
                for i in below:
                    column[i][later] = column[i][later] - lower[i][k] * factor
        write(j, solved)
        for i in range(j + 1, count):
            for k in range(8):
                upper[i] = upper[i] - lower[i][k] * u_rows[k]
                inverse[i] = inverse[i] - lower[i][k] * w_rows[k]


def kernel(a_hbm, om_hbm, map_ref, out_ref, *scratch):
    left = iter(scratch)

    def take(count):
        return [next(left) for _ in range(count)]

    a_v, om_v, part, tab_v, tab_s, all_v, mine, gram, a, v = take(10)
    a_sem, om_sem, tab_sem, tab_ss, tab_rs = take(5)
    x_ss, x_rs, c_ss, c_rs, z_ss, z_rs, f_ss, f_rs, y_ss, y_rs, s_ss, s_rs, w_ss, w_rs = take(14)
    stage_refs = [take(5) for _ in STAGES]
    part_refs = [take(14) for _ in PARTS]

    front = lax.axis_index("front")
    sibling, core = lax.rem(front, 4), lax.rem(front, 2)
    row, rows = around("row")
    col, cols = around("col")
    near = [flip(front, bits) for bits in range(4)]
    spots = [(i, j) for i in range(4) for j in range(4)]
    pending = []

    def note(copy):
        pending.append(copy)
        return copy

    barrier = pltpu.get_barrier_semaphore()
    peers = [{"row": rows[i], "col": cols[j]} for i, j in spots[1:]]
    peers += [{"front": near[1], "row": rows[i], "col": cols[j]} for i, j in spots]
    peers += [{"front": near[2]}, {"front": near[3]}]
    for where in peers:
        pl.semaphore_signal(barrier, inc=1, device_id=where, device_id_type=MESH)

    a_copies, om_copies = [], []

    def load_om(h):
        lanes = slice(HALF * h, HALF * h + HALF)
        copy = pltpu.make_async_copy(om_hbm.at[:, lanes], om_v.at[:, lanes], om_sem.at[h])
        copy.start()
        om_copies.append(copy)

    def load_a(s):
        i = len(a_copies)
        copy = pltpu.make_async_copy(
            a_hbm.at[:, pl.ds(pl.multiple_of(s * SUB, SUB), SUB), :], a_v.at[i], a_sem.at[i]
        )
        copy.start()
        a_copies.append(copy)

    load_om(0)
    load_a(cols[2])
    load_om(1)
    for s in (cols[1], cols[3], col):
        load_a(s)

    lane = lax.broadcasted_iota(jnp.int32, (8, BLK), 1)
    table = jnp.full((8, BLK), SRC, jnp.int32)
    for b in range(SRC):
        table = jnp.where(lane == map_ref[0, row * SRC + b], b, table)
    tab_v[0] = table
    for refs, (_, _, width) in zip(stage_refs, STAGES):
        for gat in refs[:2]:
            for k in range(4):
                gat[k, SRC] = jnp.zeros((8, width), jnp.float32)

    def multiply(i, h):
        product = jnp.dot(
            a_v[i].reshape(SRC * SUB, a_v.shape[-1]),
            om_v[:, HALF * h : HALF * h + HALF],
            preferred_element_type=jnp.float32,
        ).reshape(SRC, 4, 8, HALF)
        for q in range(4):
            part[i, h, q] = product[:, q]

    x_copy, c_copy, z_copy, f_copy, y_copy = {}, {}, {}, {}, {}

    def piece(i, h, t):
        q, lo, width = STAGES[t]
        return (i, h, q, slice(None), slice(None), slice(lo, lo + width))

    def send_x(t, d, step):
        i, h = ((0, d), (1 + d, 1 - d), (1 + d, d))[step]
        x_copy[t, d, step] = note(
            remote(
                part.at[piece(i, h, t)], stage_refs[t][2].at[d, step],
                x_ss.at[t, d, step], x_rs.at[t, d, step], col=cols[1] if d == 0 else cols[3],
            )
        )

    def pass_x(t):
        for d in (0, 1):
            x_copy[t, d, 0].wait_recv()
            at = piece(1 + d, d, t)
            part[at] = part[at] + stage_refs[t][2][d, 0]
            send_x(t, d, 2)

    def finish_x(t):
        for h in (0, 1):
            gat, got = stage_refs[t][h], stage_refs[t][2]
            x_copy[t, h, 2].wait_recv()
            x_copy[t, 1 - h, 1].wait_recv()
            gat[0, :SRC] = part[piece(3, h, t)] + (got[h, 2] + got[1 - h, 1])
            z_copy[t, h] = note(
                remote(gat.at[0, :SRC], gat.at[2, :SRC], z_ss.at[t, h], z_rs.at[t, h], front=near[2])
            )
            c_copy[t, h] = note(
                remote(gat.at[0, :SRC], gat.at[1, :SRC], c_ss.at[t, h], c_rs.at[t, h], front=near[1])
            )

    def forward_z(t):
        for h in (0, 1):
            gat = stage_refs[t][h]
            z_copy[t, h].wait_recv()
            f_copy[t, h] = note(
                remote(gat.at[2, :SRC], gat.at[3, :SRC], f_ss.at[t, h], f_rs.at[t, h], front=near[1])
            )

    def merge(t):
        for h in (0, 1):
            gat, _, ys, yr = stage_refs[t][h], *stage_refs[t][2:]
            c_copy[t, h].wait_recv()
            f_copy[t, h].wait_recv()
            for j in range(4 * OWN):
                at = sibling * (4 * OWN) + j
                ys[h, j] = (gat[0, tab_s[0, 0, at]] + gat[1, tab_s[1, 0, at]]) + (
                    gat[2, tab_s[2, 0, at]] + gat[3, tab_s[3, 0, at]]
                )
            for k in (1, 2, 3):
                y_copy[t, h, k] = note(
                    remote(
                        ys.at[h, pl.ds(OWN * rows[k], OWN)], yr.at[h, k - 1],
                        y_ss.at[t, h, k - 1], y_rs.at[t, h, k - 1], row=rows[k],
                    )
                )

    def finish_y(t):
        q, lo, width = STAGES[t]
        for h in (0, 1):
            _, ys, yr = stage_refs[t][2:]
            for k in (1, 2, 3):
                y_copy[t, h, k].wait_recv()
            all_v[:, col, 8 * q : 8 * q + 8, HALF * h + lo : HALF * h + lo + width] = (
                ys[h, pl.ds(OWN * row, OWN)] + yr[h, 0]
            ) + (yr[h, 1] + yr[h, 2])

    om_copies[0].wait()
    a_copies[0].wait()
    multiply(0, 0)
    pl.semaphore_wait(barrier, len(peers))
    send_x(0, 0, 0)
    send_x(1, 0, 0)
    om_copies[1].wait()
    multiply(0, 1)
    send_x(0, 1, 0)
    send_x(1, 1, 0)
    tab_copies = [
        remote(tab_v.at[0], tab_v.at[k], tab_ss.at[k - 1], tab_rs.at[k - 1], front=near[k]) for k in (1, 2, 3)
    ]
    a_copies[1].wait()
    multiply(1, 1)
    send_x(0, 0, 1)
    a_copies[2].wait()
    multiply(2, 0)
    send_x(0, 1, 1)
    multiply(1, 0)
    multiply(2, 1)
    a_copies[3].wait()
    count = len(STAGES)
    s_copy, w_copy = {}, {}

    def share_out(e, at):
        for d in (0, 1):
            block = all_v.at[:, col, at, :]
            s_copy[e, d] = note(
                remote(block, block, s_ss.at[e, d], s_rs.at[e, d], col=cols[1] if d == 0 else cols[3])
            )

    def pass_on(e, at):
        for d in (0, 1):
            s_copy[e, d].wait_recv()
            block = all_v.at[:, cols[3] if d == 0 else cols[1], at, HALF * d : HALF * d + HALF]
            w_copy[e, d] = note(
                remote(block, block, w_ss.at[e, d], w_rs.at[e, d], col=cols[1] if d == 0 else cols[3])
            )

    early, late = slice(0, 24), slice(24, 32)

    def add_gram(at, first):
        s = all_v[:, col, at, :].reshape(-1, 4 * BLK)
        base = 0
        for i in range(4):
            panel = dot(s[:, BLK * i : BLK * i + BLK], s[:, BLK * i :], ((0,), (0,)))
            for k in range(4 - i):
                block = panel[:, BLK * k : BLK * k + BLK]
                mine[base : base + BLK] = block if first else mine[base : base + BLK] + block
                base += BLK

    for tick in range(count + 4):
        if tick < count:
            pass_x(tick)
            for d in (0, 1):
                if tick + 2 < count:
                    send_x(tick + 2, d, 0)
                if tick + 1 < count:
                    send_x(tick + 1, d, 1)
        if tick == 0:
            multiply(3, 0)
            multiply(3, 1)
            for copy in tab_copies:
                copy.wait()
            tab_copy = pltpu.make_async_copy(tab_v, tab_s, tab_sem)
            tab_copy.start()
            tab_copy.wait()
        for action, lag in ((finish_x, 1), (forward_z, 2), (merge, 3), (finish_y, 4)):
            if 0 <= tick - lag < count:
                action(tick - lag)
        if tick - 4 == 2:
            share_out(0, early)
            add_gram(early, True)
    add_gram(late, False)

    def keep_rows(p):
        base, size = PARTS[p]
        half = size // 2
        return half, half // 16, lambda k: pl.ds(pl.multiple_of(base + half * k, 8), half)

    c1, yx, zz, bc = {}, {}, {}, {}
    for p in range(2):
        r1, ss, rs = part_refs[p][0], part_refs[p][5], part_refs[p][6]
        _, _, keep = keep_rows(p)
        c1[p] = note(remote(mine.at[keep(1 - core)], r1, ss, rs, front=near[1]))
    for p in range(2):
        r1, a1, r2 = part_refs[p][:3]
        ss, rs = part_refs[p][7:9]
        _, size, keep = keep_rows(p)
        c1[p].wait_recv()
        a1[...] = mine[keep(core)] + r1[...]
        for e, (i, j) in enumerate(spots[1:]):
            at = pl.ds(pl.multiple_of(size * (4 * rows[i] + cols[j]), 8), size)
            yx[p, e] = note(remote(a1.at[at], r2.at[e], ss.at[e], rs.at[e], row=rows[i], col=cols[j]))
    share_out(1, late)
    for p in range(2):
        _, a1, r2, a2, r3 = part_refs[p][:5]
        ss, rs = part_refs[p][9:11]
        _, size, _ = keep_rows(p)
        total = a1[pl.ds(pl.multiple_of(size * (4 * row + col), 8), size)]
        for e in range(15):
            yx[p, e].wait_recv()
            total = total + r2[e]
        a2[...] = total
        zz[p] = note(remote(a2, r3, ss, rs, front=near[2]))
    for p in range(2):
        a2, r3 = part_refs[p][3:5]
        ss, rs = part_refs[p][11:13]
        half, size, _ = keep_rows(p)
        base = PARTS[p][0]
        zz[p].wait_recv()
        at = pl.ds(pl.multiple_of(base + half * core + size * (4 * row + col), 8), size)
        gram[at] = a2[...] + r3[...]
        for e, (i, j) in enumerate(spots[1:]):
            bc[p, e] = note(
                remote(gram.at[at], gram.at[at], ss.at[e], rs.at[e], row=rows[i], col=cols[j])
            )
        if p == 1:
            for e, (i, j) in enumerate(spots):
                bc[p, 15 + e] = note(
                    remote(
                        gram.at[at], gram.at[at], ss.at[15 + e], rs.at[15 + e],
                        front=near[1], row=rows[i], col=cols[j],
                    )
                )
    for e in range(15):
        bc[0, e].wait_recv()
    _, _, keep = keep_rows(0)
    ends = part_refs[0][13]
    swap = note(remote(gram.at[keep(core)], gram.at[keep(core)], ends.at[0], ends.at[1], front=near[1]))
    pass_on(0, early)
    pass_on(1, late)
    swap.wait_recv()

    def unpack(p, panels):
        base = PARTS[p][0]
        for i in panels:
            for k in range(i, 4):
                a[i, :, BLK * k : BLK * k + BLK] = gram[base : base + BLK]
                base += BLK

    unpack(0, (0,))
    v[...] = jnp.zeros_like(v)
    for j in range(4):
        here = slice(BLK * j, BLK * j + BLK)

        def read(i):
            return a[j, 8 * i : 8 * i + 8, here]

        def write(i, block):
            v[j, 8 * i : 8 * i + 8, here] = block

        factor_inverse(read, write)
        if j == 0:
            for e in range(31):
                bc[1, e].wait_recv()
            unpack(1, (1, 2, 3))
        w = v[j, :, here]
        if j:
            v[j, :, : BLK * j] = dot(w, v[j, :, : BLK * j], ((1,), (0,)))
        if j < 3:
            u = dot(w, a[j, :, BLK * (j + 1) :], ((1,), (0,)))
            for i in range(j + 1, 4):
                part_u = u[:, BLK * (i - j - 1) : BLK * (i - j)]
                a[i, :, BLK * i :] = a[i, :, BLK * i :] - dot(part_u, u[:, BLK * (i - j - 1) :], ((0,), (0,)))
                v[i, :, : BLK * (j + 1)] = v[i, :, : BLK * (j + 1)] - dot(
                    part_u, v[j, :, : BLK * (j + 1)], ((0,), (0,))
                )
    for e in (0, 1):
        for d in (0, 1):
            w_copy[e, d].wait_recv()
    out_ref[...] = dot(v[col], all_v[...].reshape(OWN * BLK, 4 * BLK), ((1,), (1,)))
    for copy in pending:
        copy.wait_send()


def shards(child_blocks, sketch, block_map):
    f32, dma = jnp.float32, pltpu.SemaphoreType.DMA
    depth, width = sketch.shape
    count = len(STAGES)
    scratch = [
        pltpu.VMEM((4, SRC, SUB, depth), jnp.bfloat16),
        pltpu.VMEM((depth, width), jnp.bfloat16),
        pltpu.VMEM((4, 2, 4, SRC, 8, HALF), f32),
        pltpu.VMEM((4, 8, BLK), jnp.int32),
        pltpu.SMEM((4, 8, BLK), jnp.int32),
        pltpu.VMEM((OWN, 4, SUB, width), f32),
        pltpu.VMEM((10 * BLK, BLK), f32),
        pltpu.VMEM((10 * BLK, BLK), f32),
        pltpu.VMEM((4, BLK, width), f32),
        pltpu.VMEM((4, BLK, width), f32),
        dma((4,)), dma((2,)), dma, dma((3,)), dma((3,)),
        dma((count, 2, 3)), dma((count, 2, 3)),
    ]
    scratch += [dma((count, 2))] * 6 + [dma((count, 2, 3))] * 2 + [dma((2, 2))] * 4
    for _, _, w in STAGES:
        scratch += [
            pltpu.VMEM((4, SRC + 1, 8, w), f32),
            pltpu.VMEM((4, SRC + 1, 8, w), f32),
            pltpu.VMEM((2, 3, SRC, 8, w), f32),
            pltpu.VMEM((2, 4 * OWN, 8, w), f32),
            pltpu.VMEM((2, 3, OWN, 8, w), f32),
        ]
    for p, (_, size) in enumerate(PARTS):
        small = size // 32
        scratch += [
            pltpu.VMEM((size // 2, BLK), f32),
            pltpu.VMEM((size // 2, BLK), f32),
            pltpu.VMEM((15, small, BLK), f32),
            pltpu.VMEM((small, BLK), f32),
            pltpu.VMEM((small, BLK), f32),
            dma, dma, dma((15,)), dma((15,)), dma, dma, dma((31,)), dma((31,)), dma((2,)),
        ]
    return pl.pallas_call(
        kernel,
        out_shape=jax.ShapeDtypeStruct((BLK, OWN * BLK), f32),
        in_specs=[
            pl.BlockSpec(memory_space=pl.ANY),
            pl.BlockSpec(memory_space=pl.ANY),
            pl.BlockSpec(memory_space=pltpu.SMEM),
        ],
        out_specs=pl.BlockSpec(memory_space=pltpu.VMEM),
        scratch_shapes=scratch,
        compiler_params=pltpu.CompilerParams(collective_id=0, has_side_effects=True, vmem_limit_bytes=67043328),
        name="sketch_basis",
    )(child_blocks.reshape(SRC, BLK, depth), sketch, block_map)


def solution(mesh):
    placed = (P(("front", "row"), "col"), P("col", None), P("front", None))
    return jax.shard_map(
        shards, mesh=mesh, in_specs=placed, out_specs=P("col", ("front", "row")), check_vma=False
    )
```

time: 446 us -> 103 us (0.23); the launches traced: 437 us -> 103 us
  waiting for transfers between devices: 147 us -> 0 us
  other arithmetic: 130 us -> 0 us
  Pallas kernels: 0 us -> 101 us
  blocking collectives: 72.5 us -> 0 us
  matrix products: 33.8 us -> 0 us
  local copies, waits for them, and re-layouts: 25.1 us -> 1.77 us
  between operations: 16.9 us -> 0.01 us
  starting transfers between devices: 12.2 us -> 0 us
    another operation x22 -> x0, other arithmetic: 121 us -> none  [the longest x14 78.7 us: shards(): lower = jnp.linalg.cholesky(gram)]
    pallas_call x0 -> x1, Pallas kernels: none -> 101 us  [shards(): pl.pallas_call(kernel, out_shape=jax.ShapeDtypeStruct((BLK, OWN * BLK), f...]
    all_to_all x2 -> x0, blocking collectives: 72.5 us -> none  [from_everyone(): lax.all_to_all(jnp.broadcast_to(array[None], (count, *array.shape)), axis...]
    reduce_scatter x1 -> x0, waiting for transfers between devices: 53.2 us -> none  [shards(): lax.psum_scatter(lax.dot_general(sketch, child_blocks, (((0,), (1,)), (()...]
    all_gather x1 -> x0, waiting for transfers between devices: 48.5 us -> none  [shards(): rows_all = lax.all_gather(sketch_part, 'row', axis=1, tiled=True)]
    ppermute x10 -> x0, waiting for transfers between devices: 45 us -> none  [from_partner(): lax.ppermute(array, axis, [(i, i ^ 1 << stride) for i in range(lax.axis_s...]
    dot_general x14 -> x0, matrix products: 20.3 us -> none  [the longest x1 9.59 us: shards(): lax.dot_general(sketch, child_blocks, (((0,), (1,)), ((), ())), preferred...]
    another operation x17 -> x0, local copies, waits for them, and re-layouts: 14.3 us -> none
  transfers between devices with their start and end apart: 12 -> 0, of which waited for: 7 -> 0; matrix products, arithmetic and copies ran while one was open for 3% -> 0% of each run, Pallas kernels for 0% -> 0%
where the time goes in v2:
time: 103 us
  Pallas kernels  101 us (98%)
  local copies, waits for them, and re-layouts  1.77 us (2%)
    pallas_call x1, Pallas kernels, shards(): pl.pallas_call(kernel, out_shape=jax.ShapeDtypeStruct((BLK, OWN * BLK), f...  101 us

profile of v2, /device:TPU:1, one launch (start us, length us, event | category | flops | bytes accessed | tf_op | source)
XLA Modules:
  0.0 102.7 jit_solution(13543261376549855018)
XLA Ops:
  0.0 100.9 %sketch_basis.1 = f32[128,768]{1,0:T(8,128)} custom-call(bf16[16,128,2048]{2,1,0:T(8,128)(2,1)} %bitcast.1, bf16[2048,512]{1,0:T(8,128)(2,1)} %om_hbm.1, s32[1,64]{1,0:T(1,128)} %map_ref.1), custom_call_target="tpu_custom_call" | custom-call | tf_op jit(solution)/shard_map/sketch_basis/pallas_call | solution.py:443
  100.9 1.8 %copy.5 = f32[128,768]{1,0:T(8,128)} copy(f32[128,768]{1,0:T(8,128)} %sketch_basis.1) | data formatting | bytes 786432

commit v3 on v2

--- a/solution.py
+++ b/solution.py
@@ -12,7 +12,8 @@
 SRC = 16
 OWN = 6
 HALF = 256
-STAGES = [(0, 0, 256), (1, 0, 256), (2, 0, 256), (3, 0, 128), (3, 128, 128)]
+STAGES = [(0, 0, 256), (1, 0, 256), (2, 0, 128), (2, 128, 128), (3, 0, 128), (3, 128, 128)]
+ORDER = "p0 m p1 x0 p2 x1 f0 e0 p3 x2 p4 f1 x3 e1 y0 f2 p5 e2 x4 f3 e3 x5 y1 f4 y2 e4 f5 y3 s e5 g y4 y5".split()
 PARTS = ((0, 4 * BLK), (4 * BLK, 6 * BLK))
 
 
@@ -22,6 +23,10 @@
     )
     copy.start()
     return copy
+
+
+def settle(sem, like):
+    pltpu.make_async_copy(like, like, sem).wait()
 
 
 def around(axis):
@@ -91,9 +96,9 @@
 
     a_v, om_v, part, tab_v, tab_s, all_v, mine, gram, a, v = take(10)
     a_sem, om_sem, tab_sem, tab_ss, tab_rs = take(5)
-    x_ss, x_rs, c_ss, c_rs, z_ss, z_rs, f_ss, f_rs, y_ss, y_rs, s_ss, s_rs, w_ss, w_rs = take(14)
+    x_ss, m_rs, x_rs, g_ss, z_rs, g_rs, y_ss, y_rs, s_ss, s_rs, w_ss, w_rs = take(12)
     stage_refs = [take(5) for _ in STAGES]
-    part_refs = [take(14) for _ in PARTS]
+    part_refs = [take(15) for _ in PARTS]
 
     front = lax.axis_index("front")
     sibling, core = lax.rem(front, 4), lax.rem(front, 2)
@@ -101,11 +106,6 @@
     col, cols = around("col")
     near = [flip(front, bits) for bits in range(4)]
     spots = [(i, j) for i in range(4) for j in range(4)]
-    pending = []
-
-    def note(copy):
-        pending.append(copy)
-        return copy
 
     barrier = pltpu.get_barrier_semaphore()
     peers = [{"row": rows[i], "col": cols[j]} for i, j in spots[1:]]
@@ -132,9 +132,6 @@
 
     load_om(0)
     load_a(cols[2])
-    load_om(1)
-    for s in (cols[1], cols[3], col):
-        load_a(s)
 
     lane = lax.broadcasted_iota(jnp.int32, (8, BLK), 1)
     table = jnp.full((8, BLK), SRC, jnp.int32)
@@ -155,79 +152,72 @@
         for q in range(4):
             part[i, h, q] = product[:, q]
 
-    x_copy, c_copy, z_copy, f_copy, y_copy = {}, {}, {}, {}, {}
-
     def piece(i, h, t):
         q, lo, width = STAGES[t]
         return (i, h, q, slice(None), slice(None), slice(lo, lo + width))
 
     def send_x(t, d, step):
         i, h = ((0, d), (1 + d, 1 - d), (1 + d, d))[step]
-        x_copy[t, d, step] = note(
-            remote(
-                part.at[piece(i, h, t)], stage_refs[t][2].at[d, step],
-                x_ss.at[t, d, step], x_rs.at[t, d, step], col=cols[1] if d == 0 else cols[3],
-            )
+        remote(
+            part.at[piece(i, h, t)], stage_refs[t][2].at[step, d],
+            x_ss.at[t], (x_rs if step else m_rs).at[t], col=cols[1] if d == 0 else cols[3],
         )
 
     def pass_x(t):
+        got = stage_refs[t][2]
+        settle(m_rs.at[t], got.at[0])
         for d in (0, 1):
-            x_copy[t, d, 0].wait_recv()
             at = piece(1 + d, d, t)
-            part[at] = part[at] + stage_refs[t][2][d, 0]
+            part[at] = part[at] + got[0, d]
             send_x(t, d, 2)
+        for step, after in ((1, t + 1), (0, t + 2)):
+            if after < len(STAGES):
+                for d in (0, 1):
+                    send_x(after, d, step)
 
     def finish_x(t):
-        for h in (0, 1):
-            gat, got = stage_refs[t][h], stage_refs[t][2]
-            x_copy[t, h, 2].wait_recv()
-            x_copy[t, 1 - h, 1].wait_recv()
-            gat[0, :SRC] = part[piece(3, h, t)] + (got[h, 2] + got[1 - h, 1])
-            z_copy[t, h] = note(
-                remote(gat.at[0, :SRC], gat.at[2, :SRC], z_ss.at[t, h], z_rs.at[t, h], front=near[2])
-            )
-            c_copy[t, h] = note(
-                remote(gat.at[0, :SRC], gat.at[1, :SRC], c_ss.at[t, h], c_rs.at[t, h], front=near[1])
-            )
-
-    def forward_z(t):
+        got = stage_refs[t][2]
+        settle(x_rs.at[t], got.at[1:3])
         for h in (0, 1):
             gat = stage_refs[t][h]
-            z_copy[t, h].wait_recv()
-            f_copy[t, h] = note(
-                remote(gat.at[2, :SRC], gat.at[3, :SRC], f_ss.at[t, h], f_rs.at[t, h], front=near[1])
-            )
+            gat[0, :SRC] = part[piece(3, h, t)] + (got[2, h] + got[1, 1 - h])
+            remote(gat.at[0, :SRC], gat.at[2, :SRC], g_ss.at[t], z_rs.at[t], front=near[2])
+            remote(gat.at[0, :SRC], gat.at[1, :SRC], g_ss.at[t], g_rs.at[t], front=near[1])
+
+    def forward_z(t):
+        settle(z_rs.at[t], stage_refs[t][2].at[0])
+        for h in (0, 1):
+            gat = stage_refs[t][h]
+            remote(gat.at[2, :SRC], gat.at[3, :SRC], g_ss.at[t], g_rs.at[t], front=near[1])
 
     def merge(t):
+        settle(g_rs.at[t], stage_refs[t][2].at[1:3])
         for h in (0, 1):
-            gat, _, ys, yr = stage_refs[t][h], *stage_refs[t][2:]
-            c_copy[t, h].wait_recv()
-            f_copy[t, h].wait_recv()
+            gat, ys, yr = stage_refs[t][h], *stage_refs[t][3:]
             for j in range(4 * OWN):
                 at = sibling * (4 * OWN) + j
                 ys[h, j] = (gat[0, tab_s[0, 0, at]] + gat[1, tab_s[1, 0, at]]) + (
                     gat[2, tab_s[2, 0, at]] + gat[3, tab_s[3, 0, at]]
                 )
             for k in (1, 2, 3):
-                y_copy[t, h, k] = note(
-                    remote(
-                        ys.at[h, pl.ds(OWN * rows[k], OWN)], yr.at[h, k - 1],
-                        y_ss.at[t, h, k - 1], y_rs.at[t, h, k - 1], row=rows[k],
-                    )
+                remote(
+                    ys.at[h, pl.ds(OWN * rows[k], OWN)], yr.at[h, k - 1], y_ss.at[t], y_rs.at[t], row=rows[k]
                 )
 
     def finish_y(t):
         q, lo, width = STAGES[t]
+        ys, yr = stage_refs[t][3:]
+        settle(y_rs.at[t], yr)
         for h in (0, 1):
-            _, ys, yr = stage_refs[t][2:]
-            for k in (1, 2, 3):
-                y_copy[t, h, k].wait_recv()
             all_v[:, col, 8 * q : 8 * q + 8, HALF * h + lo : HALF * h + lo + width] = (
                 ys[h, pl.ds(OWN * row, OWN)] + yr[h, 0]
             ) + (yr[h, 1] + yr[h, 2])
 
     om_copies[0].wait()
     a_copies[0].wait()
+    load_om(1)
+    for s in (cols[1], cols[3], col):
+        load_a(s)
     multiply(0, 0)
     pl.semaphore_wait(barrier, len(peers))
     send_x(0, 0, 0)
@@ -236,9 +226,8 @@
     multiply(0, 1)
     send_x(0, 1, 0)
     send_x(1, 1, 0)
-    tab_copies = [
-        remote(tab_v.at[0], tab_v.at[k], tab_ss.at[k - 1], tab_rs.at[k - 1], front=near[k]) for k in (1, 2, 3)
-    ]
+    for k in (1, 2, 3):
+        remote(tab_v.at[0], tab_v.at[k], tab_ss, tab_rs, front=near[k])
     a_copies[1].wait()
     multiply(1, 1)
     send_x(0, 0, 1)
@@ -248,23 +237,17 @@
     multiply(1, 0)
     multiply(2, 1)
     a_copies[3].wait()
-    count = len(STAGES)
-    s_copy, w_copy = {}, {}
 
     def share_out(e, at):
         for d in (0, 1):
             block = all_v.at[:, col, at, :]
-            s_copy[e, d] = note(
-                remote(block, block, s_ss.at[e, d], s_rs.at[e, d], col=cols[1] if d == 0 else cols[3])
-            )
+            remote(block, block, s_ss.at[e], s_rs.at[e], col=cols[1] if d == 0 else cols[3])
 
     def pass_on(e, at):
+        settle(s_rs.at[e], all_v.at[:, 0:2, at, :])
         for d in (0, 1):
-            s_copy[e, d].wait_recv()
             block = all_v.at[:, cols[3] if d == 0 else cols[1], at, HALF * d : HALF * d + HALF]
-            w_copy[e, d] = note(
-                remote(block, block, w_ss.at[e, d], w_rs.at[e, d], col=cols[1] if d == 0 else cols[3])
-            )
+            remote(block, block, w_ss.at[e], w_rs.at[e], col=cols[1] if d == 0 else cols[3])
 
     early, late = slice(0, 24), slice(24, 32)
 
@@ -278,28 +261,21 @@
                 mine[base : base + BLK] = block if first else mine[base : base + BLK] + block
                 base += BLK
 
-    for tick in range(count + 4):
-        if tick < count:
-            pass_x(tick)
-            for d in (0, 1):
-                if tick + 2 < count:
-                    send_x(tick + 2, d, 0)
-                if tick + 1 < count:
-                    send_x(tick + 1, d, 1)
-        if tick == 0:
-            multiply(3, 0)
-            multiply(3, 1)
-            for copy in tab_copies:
-                copy.wait()
-            tab_copy = pltpu.make_async_copy(tab_v, tab_s, tab_sem)
-            tab_copy.start()
-            tab_copy.wait()
-        for action, lag in ((finish_x, 1), (forward_z, 2), (merge, 3), (finish_y, 4)):
-            if 0 <= tick - lag < count:
-                action(tick - lag)
-        if tick - 4 == 2:
-            share_out(0, early)
-            add_gram(early, True)
+    def own_rows():
+        multiply(3, 0)
+        multiply(3, 1)
+        settle(tab_rs, tab_v.at[1:4])
+        tab_copy = pltpu.make_async_copy(tab_v, tab_s, tab_sem)
+        tab_copy.start()
+        tab_copy.wait()
+
+    work = {"p": pass_x, "x": finish_x, "f": forward_z, "e": merge, "y": finish_y}
+    other = {"m": own_rows, "s": lambda: share_out(0, early), "g": lambda: add_gram(early, True)}
+    for item in ORDER:
+        if item in other:
+            other[item]()
+        else:
+            work[item[0]](int(item[1:]))
     add_gram(late, False)
 
     def keep_rows(p):
@@ -307,59 +283,50 @@
         half = size // 2
         return half, half // 16, lambda k: pl.ds(pl.multiple_of(base + half * k, 8), half)
 
-    c1, yx, zz, bc = {}, {}, {}, {}
     for p in range(2):
-        r1, ss, rs = part_refs[p][0], part_refs[p][5], part_refs[p][6]
+        r1, ss, rs = part_refs[p][0], *part_refs[p][5:7]
         _, _, keep = keep_rows(p)
-        c1[p] = note(remote(mine.at[keep(1 - core)], r1, ss, rs, front=near[1]))
+        remote(mine.at[keep(1 - core)], r1, ss, rs, front=near[1])
     for p in range(2):
         r1, a1, r2 = part_refs[p][:3]
         ss, rs = part_refs[p][7:9]
         _, size, keep = keep_rows(p)
-        c1[p].wait_recv()
+        settle(part_refs[p][6], r1)
         a1[...] = mine[keep(core)] + r1[...]
         for e, (i, j) in enumerate(spots[1:]):
             at = pl.ds(pl.multiple_of(size * (4 * rows[i] + cols[j]), 8), size)
-            yx[p, e] = note(remote(a1.at[at], r2.at[e], ss.at[e], rs.at[e], row=rows[i], col=cols[j]))
-    share_out(1, late)
+            remote(a1.at[at], r2.at[e], ss, rs, row=rows[i], col=cols[j])
     for p in range(2):
         _, a1, r2, a2, r3 = part_refs[p][:5]
         ss, rs = part_refs[p][9:11]
         _, size, _ = keep_rows(p)
+        settle(part_refs[p][8], r2)
         total = a1[pl.ds(pl.multiple_of(size * (4 * row + col), 8), size)]
         for e in range(15):
-            yx[p, e].wait_recv()
             total = total + r2[e]
         a2[...] = total
-        zz[p] = note(remote(a2, r3, ss, rs, front=near[2]))
+        remote(a2, r3, ss, rs, front=near[2])
     for p in range(2):
         a2, r3 = part_refs[p][3:5]
         ss, rs = part_refs[p][11:13]
         half, size, _ = keep_rows(p)
         base = PARTS[p][0]
-        zz[p].wait_recv()
+        settle(part_refs[p][10], r3)
         at = pl.ds(pl.multiple_of(base + half * core + size * (4 * row + col), 8), size)
         gram[at] = a2[...] + r3[...]
-        for e, (i, j) in enumerate(spots[1:]):
-            bc[p, e] = note(
-                remote(gram.at[at], gram.at[at], ss.at[e], rs.at[e], row=rows[i], col=cols[j])
-            )
+        for i, j in spots[1:]:
+            remote(gram.at[at], gram.at[at], ss, rs, row=rows[i], col=cols[j])
         if p == 1:
-            for e, (i, j) in enumerate(spots):
-                bc[p, 15 + e] = note(
-                    remote(
-                        gram.at[at], gram.at[at], ss.at[15 + e], rs.at[15 + e],
-                        front=near[1], row=rows[i], col=cols[j],
-                    )
-                )
-    for e in range(15):
-        bc[0, e].wait_recv()
+            for i, j in spots:
+                remote(gram.at[at], gram.at[at], ss, rs, front=near[1], row=rows[i], col=cols[j])
+    share_out(1, late)
+    settle(part_refs[0][12], part_refs[0][2])
     _, _, keep = keep_rows(0)
-    ends = part_refs[0][13]
-    swap = note(remote(gram.at[keep(core)], gram.at[keep(core)], ends.at[0], ends.at[1], front=near[1]))
+    swap_ss, swap_rs = part_refs[0][13:]
+    remote(gram.at[keep(core)], gram.at[keep(core)], swap_ss, swap_rs, front=near[1])
     pass_on(0, early)
-    pass_on(1, late)
-    swap.wait_recv()
+    settle(swap_rs, part_refs[0][0])
+    everywhere = mine.at[: 31 * PARTS[1][1] // 32]
 
     def unpack(p, panels):
         base = PARTS[p][0]
@@ -381,8 +348,8 @@
 
         factor_inverse(read, write)
         if j == 0:
-            for e in range(31):
-                bc[1, e].wait_recv()
+            pass_on(1, late)
+            settle(part_refs[1][12], everywhere)
             unpack(1, (1, 2, 3))
         w = v[j, :, here]
         if j:
@@ -395,12 +362,24 @@
                 v[i, :, : BLK * (j + 1)] = v[i, :, : BLK * (j + 1)] - dot(
                     part_u, v[j, :, : BLK * (j + 1)], ((0,), (0,))
                 )
-    for e in (0, 1):
-        for d in (0, 1):
-            w_copy[e, d].wait_recv()
+    for e, at in enumerate((early, late)):
+        settle(w_rs.at[e], all_v.at[:, 0, at, :])
     out_ref[...] = dot(v[col], all_v[...].reshape(OWN * BLK, 4 * BLK), ((1,), (1,)))
-    for copy in pending:
-        copy.wait_send()
+    settle(tab_ss, tab_v.at[1:4])
+    for t, refs in enumerate(stage_refs):
+        settle(x_ss.at[t], refs[2])
+        settle(g_ss.at[t], refs[2])
+        settle(y_ss.at[t], refs[4])
+    for e, at in enumerate((early, late)):
+        settle(s_ss.at[e], all_v.at[:, 0:2, at, :])
+        settle(w_ss.at[e], all_v.at[:, 0, at, :])
+    for p in range(2):
+        refs = part_refs[p]
+        settle(refs[5], refs[0])
+        settle(refs[7], refs[2])
+        settle(refs[9], refs[3])
+        settle(refs[11], everywhere if p else refs[2])
+    settle(swap_ss, part_refs[0][0])
 
 
 def shards(child_blocks, sketch, block_map):
@@ -418,15 +397,14 @@
         pltpu.VMEM((10 * BLK, BLK), f32),
         pltpu.VMEM((4, BLK, width), f32),
         pltpu.VMEM((4, BLK, width), f32),
-        dma((4,)), dma((2,)), dma, dma((3,)), dma((3,)),
-        dma((count, 2, 3)), dma((count, 2, 3)),
+        dma((4,)), dma((2,)), dma, dma, dma,
     ]
-    scratch += [dma((count, 2))] * 6 + [dma((count, 2, 3))] * 2 + [dma((2, 2))] * 4
+    scratch += [dma((count,))] * 8 + [dma((2,))] * 4
     for _, _, w in STAGES:
         scratch += [
             pltpu.VMEM((4, SRC + 1, 8, w), f32),
             pltpu.VMEM((4, SRC + 1, 8, w), f32),
-            pltpu.VMEM((2, 3, SRC, 8, w), f32),
+            pltpu.VMEM((3, 2, SRC, 8, w), f32),
             pltpu.VMEM((2, 4 * OWN, 8, w), f32),
             pltpu.VMEM((2, 3, OWN, 8, w), f32),
         ]
@@ -438,8 +416,7 @@
             pltpu.VMEM((15, small, BLK), f32),
             pltpu.VMEM((small, BLK), f32),
             pltpu.VMEM((small, BLK), f32),
-            dma, dma, dma((15,)), dma((15,)), dma, dma, dma((31,)), dma((31,)), dma((2,)),
-        ]
+        ] + [dma] * 10
     return pl.pallas_call(
         kernel,
         out_shape=jax.ShapeDtypeStruct((BLK, OWN * BLK), f32),

time: 103 us -> 95.1 us (0.923)
  Pallas kernels: 101 us -> 93.2 us
    pallas_call x1, Pallas kernels: 101 us -> 93.2 us  [shards(): pl.pallas_call(kernel, out_shape=jax.ShapeDtypeStruct((BLK, OWN * BLK), f...]
where the time goes in v3:
time: 95.1 us; the launch traced here: 95 us
  Pallas kernels  93.2 us (98%)
  local copies, waits for them, and re-layouts  1.77 us (2%)
    pallas_call x1, Pallas kernels, shards(): pl.pallas_call(kernel, out_shape=jax.ShapeDtypeStruct((BLK, OWN * BLK), f...  93.2 us

profile of v3, /device:TPU:1, one launch (start us, length us, event | category | flops | bytes accessed | tf_op | source)
XLA Modules:
  0.0 95.0 jit_solution(9550899144254525945)
XLA Ops:
  0.0 93.2 %sketch_basis.1 = f32[128,768]{1,0:T(8,128)} custom-call(bf16[16,128,2048]{2,1,0:T(8,128)(2,1)} %bitcast.1, bf16[2048,512]{1,0:T(8,128)(2,1)} %om_hbm.1, s32[1,64]{1,0:T(1,128)} %map_ref.1), custom_call_target="tpu_custom_call" | custom-call | tf_op jit(solution)/shard_map/sketch_basis/pallas_call | solution.py:420
  93.2 1.8 %copy.5 = f32[128,768]{1,0:T(8,128)} copy(f32[128,768]{1,0:T(8,128)} %sketch_basis.1) | data formatting | bytes 786432

commit v4 on v3

--- a/solution.py
+++ b/solution.py
@@ -58,12 +58,15 @@
     def spread(block, k):
         return jnp.broadcast_to(block[k : k + 1, :], (8, BLK))
 
+    def columns(block, j):
+        return [jnp.broadcast_to(block[:, 8 * j + k : 8 * j + k + 1], (8, BLK)) for k in range(8)]
+
+    ahead = columns(upper[0], 0)
     for j in range(count):
         below = range(j, count)
-        column = {
-            i: [jnp.broadcast_to(upper[i][:, 8 * j + k : 8 * j + k + 1], (8, BLK)) for k in range(8)]
-            for i in below
-        }
+        column = {i: columns(upper[i], j) for i in range(j + 1, count)}
+        column[j] = ahead
+        ahead = columns(upper[j + 1], j + 1) if j + 1 < count else []
         lower = {i: [] for i in below}
         rest, solved = upper[j], inverse[j]
         u_rows, w_rows = [], []
@@ -81,6 +84,8 @@
                 factor = spread(lower[j][k], later)
                 for i in below:
                     column[i][later] = column[i][later] - lower[i][k] * factor
+            for c in range(len(ahead)):
+                ahead[c] = ahead[c] - lower[j + 1][k] * spread(lower[j + 1][k], c)
         write(j, solved)
         for i in range(j + 1, count):
             for k in range(8):
@@ -132,6 +137,9 @@
 
     load_om(0)
     load_a(cols[2])
+    load_om(1)
+    for s in (cols[1], cols[3], col):
+        load_a(s)
 
     lane = lax.broadcasted_iota(jnp.int32, (8, BLK), 1)
     table = jnp.full((8, BLK), SRC, jnp.int32)
@@ -215,9 +223,6 @@
 
     om_copies[0].wait()
     a_copies[0].wait()
-    load_om(1)
-    for s in (cols[1], cols[3], col):
-        load_a(s)
     multiply(0, 0)
     pl.semaphore_wait(barrier, len(peers))
     send_x(0, 0, 0)

time: 95.1 us -> 91.1 us (0.958)
  Pallas kernels: 93.2 us -> 89.2 us
    pallas_call x1, Pallas kernels: 93.2 us -> 89.2 us  [shards(): pl.pallas_call(kernel, out_shape=jax.ShapeDtypeStruct((BLK, OWN * BLK), f...]
where the time goes in v4:
time: 91.1 us; the launch traced here: 90.9 us
  Pallas kernels  89.2 us (98%)
  local copies, waits for them, and re-layouts  1.77 us (2%)
    pallas_call x1, Pallas kernels, shards(): pl.pallas_call(kernel, out_shape=jax.ShapeDtypeStruct((BLK, OWN * BLK), f...  89.2 us

profile of v4, /device:TPU:1, one launch (start us, length us, event | category | flops | bytes accessed | tf_op | source)
XLA Modules:
  0.0 90.9 jit_solution(1650624458856732216)
XLA Ops:
  0.0 89.2 %sketch_basis.1 = f32[128,768]{1,0:T(8,128)} custom-call(bf16[16,128,2048]{2,1,0:T(8,128)(2,1)} %bitcast.1, bf16[2048,512]{1,0:T(8,128)(2,1)} %om_hbm.1, s32[1,64]{1,0:T(1,128)} %map_ref.1), custom_call_target="tpu_custom_call" | custom-call | tf_op jit(solution)/shard_map/sketch_basis/pallas_call | solution.py:425
  89.2 1.8 %copy.5 = f32[128,768]{1,0:T(8,128)} copy(f32[128,768]{1,0:T(8,128)} %sketch_basis.1) | data formatting | bytes 786432
